TPU v7x, 32 devices: a whole 2x2x4 slice. The times are simulated.
32 devices in a mesh: ctx: 16 (over z, y, x), head: 2 (over core).
Axes of the slice: x: 2, y: 2, z: 4, core: 2. Of those that a mesh axis runs over, the one named last changes fastest.
Arguments:
- query: bfloat16 [2048, 384], P('ctx', 'head'), may hold values from -48 to 48
- key_nope: bfloat16 [2048, 256], P('ctx', 'head'), may hold values from -8 to 8
- key_rope: bfloat16 [2048, 64], P('ctx'), may hold values from -8 to 8
- value: bfloat16 [2048, 256], P('ctx', 'head'), may hold values from -6 to 6
- d_out: bfloat16 [2048, 256], P('ctx', 'head'), may hold values from -288 to 288
- positions: int32 [2048], P('ctx'), may hold values from 0 to 2047, as said below
- segments: int32 [2048], replicated, may hold values from 0 to 3, never falling along the last dimension, each value on 1 to 1024 neighbouring positions
Outputs:
- d_query: bfloat16 [2048, 384], P('ctx', 'head')
- d_key_nope: bfloat16 [2048, 256], P('ctx', 'head')
- d_key_rope: bfloat16 [2048, 64], P('ctx')
- d_value: bfloat16 [2048, 256], P('ctx', 'head')
Inputs may be any that keep to these rules, and one draw needn't show every extreme that they name: A permutation of 0 to 2047 made of aligned blocks of 32 rows holding 32 consecutive positions in order.
All inputs are finite; a program needn't handle non-finite values.
Results may differ from a plain program's by a relative error of at most 0.0049.
Values may be sent and summed in bfloat16 or wider, within the bound.
A program may use at most 64 MiB of HBM per device.

v0:
```python
import math
import jax
import jax.numpy as jnp
from jax import lax
from jax.sharding import PartitionSpec as P

NOPE = 128
ROPE = 64
VD = 128
QK = 192
clip_ratio = 0.25
block_limit = 1024


def split_heads(array, width):
    return array.reshape(array.shape[0], -1, width)


def make_keys(nope_rows, rope_rows):
    nope_three = split_heads(nope_rows, NOPE)
    rope_three = rope_rows[:, None, :]
    return jnp.concatenate([nope_three, rope_three], axis=2)


def visible(query_place, query_doc, key_place, key_doc):
    return (query_doc[:, None] == key_doc[None, :]) & (key_place[None, :] <= query_place[:, None])


def over_blocks(advance, carried, pieces, offset=0):
    row_count = pieces[0].shape[0]
    blocks = row_count // block_limit
    parts = jax.tree.map(
        lambda array: array.reshape((blocks, block_limit) + array.shape[1:]), pieces
    )

    def visitor(state_now, part_now):
        return (advance(state_now, part_now, offset), None)

    carried, unused = lax.scan(visitor, carried, parts)
    return carried


def shards(query, key_nope, key_rope, value, d_out, positions, segments):
    softmax_scale = 1.0 / math.sqrt(QK)
    documents = jnp.take(segments, positions)
    local_rows = query.shape[0]
    heads_here = query.shape[1] // QK
    query_three = split_heads(query, QK)
    dout_three = split_heads(d_out, VD)

    def soft_advance(carried, pieces, offset):
        row_max, row_sum, weighted = carried
        piece_nope, piece_rope, piece_value, piece_place, piece_doc = pieces
        key_rows = make_keys(piece_nope, piece_rope)
        scores = (
            jnp.einsum("qhd,khd->hqk", query_three, key_rows, preferred_element_type=jnp.float32)
            * softmax_scale
        )
        allowed = visible(positions, documents, piece_place, piece_doc)[None]
        scores = jnp.where(allowed, scores, -jnp.inf)
        new_max = jnp.maximum(row_max, jnp.max(scores, axis=2))
        safe_max = jnp.where(new_max == -jnp.inf, 0.0, new_max)
        exponent = jnp.exp(scores - safe_max[:, :, None])
        d_prob = jnp.einsum(
            "qhv,khv->hqk",
            dout_three,
            split_heads(piece_value, VD),
            preferred_element_type=jnp.float32,
        )
        shrink = jnp.exp(row_max - safe_max)
        return (
            new_max,
            row_sum * shrink + jnp.sum(exponent, axis=2),
            weighted * shrink + jnp.sum(exponent * d_prob, axis=2),
        )

    soft_init = (
        jnp.full((heads_here, local_rows), -jnp.inf, jnp.float32),
        jnp.zeros((heads_here, local_rows), jnp.float32),
        jnp.zeros((heads_here, local_rows), jnp.float32),
    )
    soft_state = over_blocks(
        soft_advance,
        soft_init,
        (
            lax.all_gather(key_nope, "ctx", axis=0, tiled=True),
            lax.all_gather(key_rope, "ctx", axis=0, tiled=True),
            lax.all_gather(value, "ctx", axis=0, tiled=True),
            lax.all_gather(positions, "ctx", axis=0, tiled=True),
            lax.all_gather(documents, "ctx", axis=0, tiled=True),
        ),
        jnp.int32(0),
    )
    row_max, row_sum, weighted = soft_state
    log_total = row_max + jnp.log(row_sum)
    row_delta = weighted / row_sum

    def query_advance(grad_query, pieces, offset):
        piece_nope, piece_rope, piece_value, piece_place, piece_doc = pieces
        key_rows = make_keys(piece_nope, piece_rope)
        scores = (
            jnp.einsum("qhd,khd->hqk", query_three, key_rows, preferred_element_type=jnp.float32)
            * softmax_scale
        )
        allowed = visible(positions, documents, piece_place, piece_doc)[None]
        weights = jnp.exp(jnp.where(allowed, scores, -jnp.inf) - log_total[:, :, None])
        d_prob = jnp.einsum(
            "qhv,khv->hqk",
            dout_three,
            split_heads(piece_value, VD),
            preferred_element_type=jnp.float32,
        )
        d_score = (weights * (d_prob - row_delta[:, :, None])).astype(jnp.bfloat16)
        return (
            grad_query
            + jnp.einsum("hqk,khd->qhd", d_score, key_rows, preferred_element_type=jnp.float32)
            * softmax_scale
        )

    query_init = jnp.zeros((local_rows, heads_here, QK), jnp.float32)
    grad_query = over_blocks(
        query_advance,
        query_init,
        (
            lax.all_gather(key_nope, "ctx", axis=0, tiled=True),
            lax.all_gather(key_rope, "ctx", axis=0, tiled=True),
            lax.all_gather(value, "ctx", axis=0, tiled=True),
            lax.all_gather(positions, "ctx", axis=0, tiled=True),
            lax.all_gather(documents, "ctx", axis=0, tiled=True),
        ),
        jnp.int32(0),
    )
    local_keys = make_keys(key_nope, key_rope)
    value_three = split_heads(value, VD)

    def key_advance(carried, pieces, offset):
        grad_key, grad_value = carried
        piece_query, piece_dout, piece_log, piece_delta, piece_place, piece_doc = pieces
        piece_query_three = split_heads(piece_query, QK)
        piece_dout_three = split_heads(piece_dout, VD)
        scores = (
            jnp.einsum(
                "qhd,khd->hqk", piece_query_three, local_keys, preferred_element_type=jnp.float32
            )
            * softmax_scale
        )
        allowed = visible(piece_place, piece_doc, positions, documents)[None]
        weights = jnp.exp(jnp.where(allowed, scores, -jnp.inf) - piece_log.T[:, :, None])
        d_prob = jnp.einsum(
            "qhv,khv->hqk", piece_dout_three, value_three, preferred_element_type=jnp.float32
        )
        d_score = (weights * (d_prob - piece_delta.T[:, :, None])).astype(jnp.bfloat16)
        grad_key = (
            grad_key
            + jnp.einsum(
                "hqk,qhd->khd", d_score, piece_query_three, preferred_element_type=jnp.float32
            )
            * softmax_scale
        )
        grad_value = grad_value + jnp.einsum(
            "hqk,qhv->khv",
            weights.astype(jnp.bfloat16),
            piece_dout_three,
            preferred_element_type=jnp.float32,
        )
        return (grad_key, grad_value)

    key_init = (
        jnp.zeros((local_rows, heads_here, QK), jnp.float32),
        jnp.zeros((local_rows, heads_here, VD), jnp.float32),
    )
    grad_key, grad_value = over_blocks(
        key_advance,
        key_init,
        (
            lax.all_gather(query.astype(jnp.float32), "ctx", axis=0, tiled=True).astype(
                jnp.bfloat16
            ),
            lax.all_gather(d_out.astype(jnp.float32), "ctx", axis=0, tiled=True).astype(
                jnp.bfloat16
            ),
            lax.all_gather(log_total.T, "ctx", axis=0, tiled=True),
            lax.all_gather(row_delta.T, "ctx", axis=0, tiled=True),
            lax.all_gather(positions, "ctx", axis=0, tiled=True),
            lax.all_gather(documents, "ctx", axis=0, tiled=True),
        ),
        jnp.int32(0),
    )
    grad_nope = grad_key[:, :, :NOPE]
    rope_part = jnp.sum(grad_key[:, :, NOPE:], axis=1)
    local_squares = (
        jnp.sum(jnp.square(grad_query))
        + jnp.sum(jnp.square(grad_nope))
        + jnp.sum(jnp.square(grad_value))
    )
    rope_summed = lax.psum(rope_part, "head")
    first_head = (lax.axis_index("head") == 0).astype(jnp.float32)
    local_squares = local_squares + first_head * jnp.sum(jnp.square(rope_summed))
    total = lax.psum(local_squares, ("ctx", "head"))
    count_all = float(
        local_rows
        * lax.axis_size("ctx")
        * (heads_here * lax.axis_size("head") * (QK + NOPE + VD) + ROPE)
    )
    factor = jnp.minimum(1.0, clip_ratio * math.sqrt(count_all) / jnp.sqrt(total))
    d_key_rope = (rope_summed * factor).astype(jnp.bfloat16)
    d_query = (grad_query * factor).astype(jnp.bfloat16).reshape(local_rows, heads_here * QK)
    d_key_nope = (grad_nope * factor).astype(jnp.bfloat16).reshape(local_rows, heads_here * NOPE)
    d_value = (grad_value * factor).astype(jnp.bfloat16).reshape(local_rows, heads_here * VD)
    return (d_query, d_key_nope, d_key_rope, d_value)


def solution(mesh):
    return jax.shard_map(
        shards,
        mesh=mesh,
        in_specs=(
            P("ctx", "head"),
            P("ctx", "head"),
            P("ctx", None),
            P("ctx", "head"),
            P("ctx", "head"),
            P("ctx"),
            P(),
        ),
        out_specs=(P("ctx", "head"), P("ctx", "head"), P("ctx", None), P("ctx", "head")),
        check_vma=False,
    )
```

profile of v0, /device:TPU:12, one launch (start us, length us, event | category | flops | bytes accessed | tf_op | source)
XLA Modules:
  0.0 411.8 jit_solution(17462087313874825854)
XLA Ops:
  0.7 34.1 %all_gather.34 = bf16[2048,128]{1,0:T(8,128)(2,1)S(1)} all-gather(bf16[128,128]{1,0:T(8,128)(2,1)} %param.14), channel_id=1, replica_groups=mesh['ctx'=16,'head'=2] {'ctx'}, dimensions={0}, use_global_device_ids=true | all-gather | bytes 557056 | tf_op jit(solution)/shard_map/all_gather | solution.py:125
  34.7 37.1 %all_gather.35 = bf16[2048,64]{0,1:T(8,128)(2,1)S(1)} all-gather(bf16[128,64]{0,1:T(8,128)(2,1)S(1)} %copy-done.4), channel_id=1, replica_groups=mesh['ctx'=16,'head'=2] {'ctx'}, dimensions={0}, use_global_device_ids=true | all-gather | bytes 278528 | tf_op jit(solution)/shard_map/all_gather | solution.py:126
  72.2 0.6 copy-done.6
  72.8 1.1 gather_fusion
  74.0 37.4 %all-gather.2 = s32[16,1,128]{2,1,0:T(1,128)S(1)} all-gather(s32[1,1,128]{2,1,0:T(1,128)S(1)} %bitcast.246), channel_id=1, replica_groups=mesh['ctx'=16,'head'=2] {'ctx'}, dimensions={0}, use_global_device_ids=true | all-gather | bytes 8704 | tf_op jit(solution)/shard_map/all_gather | solution.py:129
  111.4 0.5 broadcast.162
  111.9 0.7 reduce.12
  112.6 35.7 %all-gather.3 = s32[16,1,128]{2,1,0:T(1,128)S(1)} all-gather(s32[1,1,128]{2,1,0:T(1,128)S(1)} %bitcast.245), channel_id=1, replica_groups=mesh['ctx'=16,'head'=2] {'ctx'}, dimensions={0}, use_global_device_ids=true | all-gather | bytes 8704 | tf_op jit(solution)/shard_map/all_gather | solution.py:128
  148.2 0.7 reduce.13
  149.0 40.6 %all_gather.38 = bf16[2048,128]{1,0:T(8,128)(2,1)S(1)} all-gather(bf16[128,128]{1,0:T(8,128)(2,1)S(1)} %copy-done.2), channel_id=1, replica_groups=mesh['ctx'=16,'head'=2] {'ctx'}, dimensions={0}, use_global_device_ids=true | all-gather | bytes 557056 | tf_op jit(solution)/shard_map/all_gather | solution.py:127
  189.6 2.0 while.39
  191.6 2.0 while.40
  191.9 0.7 fusion.120
  192.9 0.7 fusion.120
  193.6 0.6 multiply_reduce_fusion
  194.3 40.7 %all_gather.39 = bf16[2048,192]{0,1:T(8,128)(2,1)S(1)} all-gather(bf16[128,192]{0,1:T(8,128)(2,1)S(1)} %bitcast.242), channel_id=1, replica_groups=mesh['ctx'=16,'head'=2] {'ctx'}, dimensions={0}, use_global_device_ids=true | all-gather | bytes 835584 | tf_op jit(solution)/shard_map/all_gather | solution.py:176
  234.9 0.5 copy.24
  235.6 0.6 copy-done.3
  236.3 37.2 %all-gather = f32[1,2048]{1,0:T(1,128)S(1)} all-gather(f32[1,128]{1,0:T(1,128)S(1)} %get-tuple-element.874), channel_id=2, replica_groups=mesh['ctx'=16,'head'=2] {'ctx'}, dimensions={1}, use_global_device_ids=true | all-gather | bytes 8704 | tf_op jit(solution)/shard_map/all_gather | solution.py:182
  273.5 38.5 %all_gather.41 = bf16[2048,128]{1,0:T(8,128)(2,1)S(1)} all-gather(bf16[128,128]{1,0:T(8,128)(2,1)S(1)} %bitcast.227), channel_id=1, replica_groups=mesh['ctx'=16,'head'=2] {'ctx'}, dimensions={0}, use_global_device_ids=true | all-gather | bytes 557056 | tf_op jit(solution)/shard_map/all_gather | solution.py:179
  312.0 37.3 %all-gather.1 = f32[1,2048]{1,0:T(1,128)S(1)} all-gather(f32[1,128]{1,0:T(1,128)S(1)} %get-tuple-element.873), channel_id=3, replica_groups=mesh['ctx'=16,'head'=2] {'ctx'}, dimensions={1}, use_global_device_ids=true | all-gather | bytes 8704 | tf_op jit(solution)/shard_map/all_gather | solution.py:183
  349.2 2.7 while.41
  349.8 0.5 fusion.129
  351.1 0.5 fusion.129
  352.1 0.6 multiply_reduce_fusion.2
  354.0 0.6 multiply_reduce_fusion.1
  355.3 3.4 psum.14
  358.7 0.6 multiply_reduce_fusion.3
  360.0 49.1 %psum.15 = f32[]{:T(128)} all-reduce(f32[]{:T(128)S(6)} %add.53), channel_id=1, replica_groups=mesh['ctx'=16,'head'=2] {'ctx','head'}, use_global_device_ids=true, to_apply=%region_14.15 | all-reduce | flops 1 | bytes 8 | tf_op jit(solution)/shard_map/psum | solution.py:199
  409.8 0.6 fusion.82
  410.5 0.6 fusion.83
  411.1 0.6 multiply_convert_fusion.3
  (65 shorter events, 4.8 us)
Async XLA Ops:
  0.6 72.2 %copy-start = (s32[2048]{0:T(1024)S(1)}, s32[2048]{0:T(1024)}, u32[]{:S(2)}) copy-start(s32[2048]{0:T(1024)} %param.19) | copy-start | bytes 24580
  0.7 34.1 %copy-start.4 = (bf16[128,64]{0,1:T(8,128)(2,1)S(1)}, bf16[128,64]{0,1:T(8,128)(2,1)}, u32[]{:S(2)}) copy-start(bf16[128,64]{0,1:T(8,128)(2,1)} %param.15) | copy-start | bytes 49156
  72.2 0.7 copy-start.6
  112.5 36.4 %copy-start.2 = (bf16[128,128]{1,0:T(8,128)(2,1)S(1)}, bf16[128,128]{1,0:T(8,128)(2,1)}, u32[]{:S(2)}) copy-start(bf16[128,128]{1,0:T(8,128)(2,1)} %param.16) | copy-start | bytes 98308
  149.0 40.6 %copy-start.1 = (bf16[128,128]{1,0:T(8,128)(2,1)S(1)}, bf16[128,128]{1,0:T(8,128)(2,1)}, u32[]{:S(2)}) copy-start(bf16[128,128]{1,0:T(8,128)(2,1)} %param.17) | copy-start | bytes 98308
  149.0 40.6 %copy-start.5 = (bf16[128,192]{0,1:T(8,128)(2,1)S(1)}, bf16[128,192]{0,1:T(8,128)(2,1)}, u32[]{:S(2)}) copy-start(bf16[128,192]{0,1:T(8,128)(2,1)} %param.13) | copy-start | bytes 147460
  235.4 0.8 copy-start.3
where the time goes:
time: 412 us
  blocking collectives  391 us (95%)
  other arithmetic  6.09 us (1%)
  matrix products  5.79 us (1%)
  local copies, waits for them, and re-layouts  4.48 us (1%)
  between operations  4.17 us (1%)
    psum x1, blocking collectives, shards(): total = lax.psum(local_squares, ('ctx', 'head'))  49.1 us
    all_gather x1, blocking collectives, shards(): lax.all_gather(query.astype(jnp.float32), 'ctx', axis=0, tiled=True)  40.7 us
    all_gather x1, blocking collectives, shards(): lax.all_gather(value, 'ctx', axis=0, tiled=True)  40.6 us
    all_gather x1, blocking collectives, shards(): lax.all_gather(d_out.astype(jnp.float32), 'ctx', axis=0, tiled=True)  38.5 us
    all_gather x1, blocking collectives, shards(): lax.all_gather(documents, 'ctx', axis=0, tiled=True)  37.4 us
    all_gather x1, blocking collectives, shards(): lax.all_gather(row_delta.T, 'ctx', axis=0, tiled=True)  37.3 us
    all_gather x1, blocking collectives, shards(): lax.all_gather(log_total.T, 'ctx', axis=0, tiled=True)  37.2 us
    all_gather x1, blocking collectives, shards(): lax.all_gather(key_rope, 'ctx', axis=0, tiled=True)  37.1 us

commit v1 on v0

--- a/solution.py
+++ b/solution.py
@@ -196,7 +196,7 @@
     rope_summed = lax.psum(rope_part, "head")
     first_head = (lax.axis_index("head") == 0).astype(jnp.float32)
     local_squares = local_squares + first_head * jnp.sum(jnp.square(rope_summed))
-    total = lax.psum(local_squares, ("ctx", "head"))
+    total = lax.all_gather(local_squares, ("ctx", "head")).sum(axis=0)
     count_all = float(
         local_rows
         * lax.axis_size("ctx")

time: 412 us -> 413 us (level)
    psum x1 -> x0, blocking collectives: 49.1 us -> none  [shards(): total = lax.psum(local_squares, ('ctx', 'head'))]
    unnamed x0 -> x1, blocking collectives: none -> 48.9 us
where the time goes in v1:
time: 413 us; the launch traced here: 412 us
  blocking collectives  391 us (95%)
  other arithmetic  6.69 us (2%)
  matrix products  5.79 us (1%)
  local copies, waits for them, and re-layouts  4.6 us (1%)
  between operations  4.18 us (1%)
    unnamed x1, blocking collectives  48.9 us
    all_gather x1, blocking collectives, shards(): lax.all_gather(query.astype(jnp.float32), 'ctx', axis=0, tiled=True)  40.7 us
    all_gather x1, blocking collectives, shards(): lax.all_gather(value, 'ctx', axis=0, tiled=True)  40.6 us
    all_gather x1, blocking collectives, shards(): lax.all_gather(d_out.astype(jnp.float32), 'ctx', axis=0, tiled=True)  38.5 us
    all_gather x1, blocking collectives, shards(): lax.all_gather(documents, 'ctx', axis=0, tiled=True)  37.4 us
    all_gather x1, blocking collectives, shards(): lax.all_gather(row_delta.T, 'ctx', axis=0, tiled=True)  37.3 us
    all_gather x1, blocking collectives, shards(): lax.all_gather(log_total.T, 'ctx', axis=0, tiled=True)  37.2 us
    all_gather x1, blocking collectives, shards(): lax.all_gather(key_rope, 'ctx', axis=0, tiled=True)  37.1 us

profile of v1, /device:TPU:12, one launch (start us, length us, event | category | flops | bytes accessed | tf_op | source)
XLA Modules:
  0.0 412.2 jit_solution(13939883977414014317)
XLA Ops:
  0.7 34.1 %all_gather.40 = bf16[2048,128]{1,0:T(8,128)(2,1)S(1)} all-gather(bf16[128,128]{1,0:T(8,128)(2,1)} %param.14), channel_id=1, replica_groups=mesh['ctx'=16,'head'=2] {'ctx'}, dimensions={0}, use_global_device_ids=true | all-gather | bytes 557056 | tf_op jit(solution)/shard_map/all_gather | solution.py:125
  34.7 37.1 %all_gather.41 = bf16[2048,64]{0,1:T(8,128)(2,1)S(1)} all-gather(bf16[128,64]{0,1:T(8,128)(2,1)S(1)} %copy-done.4), channel_id=1, replica_groups=mesh['ctx'=16,'head'=2] {'ctx'}, dimensions={0}, use_global_device_ids=true | all-gather | bytes 278528 | tf_op jit(solution)/shard_map/all_gather | solution.py:126
  72.2 0.6 copy-done.6
  72.8 1.1 gather_fusion
  74.0 37.4 %all-gather.2 = s32[16,1,128]{2,1,0:T(1,128)S(1)} all-gather(s32[1,1,128]{2,1,0:T(1,128)S(1)} %bitcast.247), channel_id=1, replica_groups=mesh['ctx'=16,'head'=2] {'ctx'}, dimensions={0}, use_global_device_ids=true | all-gather | bytes 8704 | tf_op jit(solution)/shard_map/all_gather | solution.py:129
  111.4 0.5 broadcast.163
  111.9 0.7 reduce.13
  112.6 35.7 %all-gather.3 = s32[16,1,128]{2,1,0:T(1,128)S(1)} all-gather(s32[1,1,128]{2,1,0:T(1,128)S(1)} %bitcast.246), channel_id=1, replica_groups=mesh['ctx'=16,'head'=2] {'ctx'}, dimensions={0}, use_global_device_ids=true | all-gather | bytes 8704 | tf_op jit(solution)/shard_map/all_gather | solution.py:128
  148.2 0.7 reduce.14
  149.0 40.6 %all_gather.44 = bf16[2048,128]{1,0:T(8,128)(2,1)S(1)} all-gather(bf16[128,128]{1,0:T(8,128)(2,1)S(1)} %copy-done.2), channel_id=1, replica_groups=mesh['ctx'=16,'head'=2] {'ctx'}, dimensions={0}, use_global_device_ids=true | all-gather | bytes 557056 | tf_op jit(solution)/shard_map/all_gather | solution.py:127
  189.6 2.0 while.39
  191.6 2.0 while.40
  191.9 0.7 fusion.120
  192.9 0.7 fusion.120
  193.6 0.6 multiply_reduce_fusion
  194.3 40.7 %all_gather.45 = bf16[2048,192]{0,1:T(8,128)(2,1)S(1)} all-gather(bf16[128,192]{0,1:T(8,128)(2,1)S(1)} %bitcast.243), channel_id=1, replica_groups=mesh['ctx'=16,'head'=2] {'ctx'}, dimensions={0}, use_global_device_ids=true | all-gather | bytes 835584 | tf_op jit(solution)/shard_map/all_gather | solution.py:176
  235.6 0.6 copy-done.3
  236.3 37.2 %all-gather = f32[1,2048]{1,0:T(1,128)S(1)} all-gather(f32[1,128]{1,0:T(1,128)S(1)} %get-tuple-element.874), channel_id=2, replica_groups=mesh['ctx'=16,'head'=2] {'ctx'}, dimensions={1}, use_global_device_ids=true | all-gather | bytes 8704 | tf_op jit(solution)/shard_map/all_gather | solution.py:182
  273.5 38.5 %all_gather.47 = bf16[2048,128]{1,0:T(8,128)(2,1)S(1)} all-gather(bf16[128,128]{1,0:T(8,128)(2,1)S(1)} %bitcast.228), channel_id=1, replica_groups=mesh['ctx'=16,'head'=2] {'ctx'}, dimensions={0}, use_global_device_ids=true | all-gather | bytes 557056 | tf_op jit(solution)/shard_map/all_gather | solution.py:179
  312.0 37.3 %all-gather.1 = f32[1,2048]{1,0:T(1,128)S(1)} all-gather(f32[1,128]{1,0:T(1,128)S(1)} %get-tuple-element.873), channel_id=3, replica_groups=mesh['ctx'=16,'head'=2] {'ctx'}, dimensions={1}, use_global_device_ids=true | all-gather | bytes 8704 | tf_op jit(solution)/shard_map/all_gather | solution.py:183
  349.2 2.7 while.41
  349.8 0.5 fusion.129
  351.1 0.5 fusion.129
  352.1 0.6 multiply_reduce_fusion.2
  354.0 0.6 multiply_reduce_fusion.1
  355.3 3.4 psum.7
  358.7 0.6 multiply_reduce_fusion.3
  360.1 48.9 %all-reduce = f32[32]{0:T(128)S(1)} all-reduce(f32[32]{0:T(128)S(1)} %dynamic-update-slice), channel_id=1, replica_groups=mesh['ctx'=16,'head'=2] {'ctx','head'}, use_global_device_ids=true, to_apply=%add | all-reduce | flops 32 | bytes 256
  409.0 0.6 reduce_sum.78
  410.2 0.6 fusion.82
  411.0 0.6 fusion.83
  411.6 0.6 multiply_convert_fusion.3
  (68 shorter events, 5.5 us)
Async XLA Ops:
  0.6 72.2 %copy-start = (s32[2048]{0:T(1024)S(1)}, s32[2048]{0:T(1024)}, u32[]{:S(2)}) copy-start(s32[2048]{0:T(1024)} %param.19) | copy-start | bytes 24580
  0.7 34.1 %copy-start.4 = (bf16[128,64]{0,1:T(8,128)(2,1)S(1)}, bf16[128,64]{0,1:T(8,128)(2,1)}, u32[]{:S(2)}) copy-start(bf16[128,64]{0,1:T(8,128)(2,1)} %param.15) | copy-start | bytes 49156
  72.2 0.7 copy-start.6
  112.5 36.4 %copy-start.2 = (bf16[128,128]{1,0:T(8,128)(2,1)S(1)}, bf16[128,128]{1,0:T(8,128)(2,1)}, u32[]{:S(2)}) copy-start(bf16[128,128]{1,0:T(8,128)(2,1)} %param.16) | copy-start | bytes 98308
  149.0 40.6 %copy-start.1 = (bf16[128,128]{1,0:T(8,128)(2,1)S(1)}, bf16[128,128]{1,0:T(8,128)(2,1)}, u32[]{:S(2)}) copy-start(bf16[128,128]{1,0:T(8,128)(2,1)} %param.17) | copy-start | bytes 98308
  149.0 40.6 %copy-start.5 = (bf16[128,192]{0,1:T(8,128)(2,1)S(1)}, bf16[128,192]{0,1:T(8,128)(2,1)}, u32[]{:S(2)}) copy-start(bf16[128,192]{0,1:T(8,128)(2,1)} %param.13) | copy-start | bytes 147460
  235.4 0.8 copy-start.3
